TPU v7x, 32 devices: a whole 2x2x4 slice. The times are simulated.
32 devices in a mesh: row: 4 (over z), col: 4 (over x, core), depth: 2 (over y).
Axes of the slice: x: 2, y: 2, z: 4, core: 2. Of those that a mesh axis runs over, the one named last changes fastest.
Arguments:
- tokens: bfloat16 [2048, 8192], P(('row', 'col'), 'depth'), may hold values from -0.3125 to 0.3125
- weight: bfloat16 [8192, 8192], P('depth', ('col', 'row')), may hold values from -0.0625 to 0.0625
- grad_output: bfloat16 [2048, 8192], P('row', ('col', 'depth')), may hold values from -6 to 6
Outputs:
- grad_input: bfloat16 [2048, 8192], P(('row', 'col'), 'depth')
- grad_weight: bfloat16 [8192, 8192], P('depth', ('col', 'row'))
All inputs are finite; a program needn't handle non-finite values.
Results may differ from a plain program's by a relative error of at most 0.001.
Values may be sent and summed in bfloat16 or wider, within the bound.
A program may use at most 128 MiB of HBM per device.

v0:
```python
import jax
import jax.numpy as jnp
from jax import lax
from jax.sharding import PartitionSpec as P

last_with_last = (((1,), (1,)), ((), ()))
first_with_first = (((0,), (0,)), ((), ()))


def input_grads(weight, grad_block):
    weight_block = lax.all_gather(weight, "row", axis=1, tiled=True)
    partial_value = lax.dot_general(
        grad_block, weight_block, last_with_last, preferred_element_type=jnp.float32
    )
    column_slab = lax.psum_scatter(partial_value, "col", scatter_dimension=1, tiled=True).astype(
        jnp.bfloat16
    )
    return lax.all_to_all(column_slab, "col", split_axis=0, concat_axis=1, tiled=True)


def weight_grads(tokens, grad_block):
    partial_value = lax.dot_general(
        lax.all_gather(tokens, "col", axis=0, tiled=True),
        grad_block,
        first_with_first,
        preferred_element_type=jnp.float32,
    )
    return lax.psum_scatter(partial_value, "row", scatter_dimension=1, tiled=True).astype(
        jnp.bfloat16
    )


def per_device(tokens, weight, grad_output):
    grad_block = lax.all_gather(grad_output, "depth", axis=1, tiled=True)
    grad_input = input_grads(weight, grad_block)
    grad_weight = weight_grads(tokens, grad_block)
    return (grad_input, grad_weight)


def solution(mesh):
    return jax.shard_map(
        per_device,
        mesh=mesh,
        in_specs=(
            P(("row", "col"), "depth"),
            P("depth", ("col", "row")),
            P("row", ("col", "depth")),
        ),
        out_specs=(P(("row", "col"), "depth"), P("depth", ("col", "row"))),
        check_vma=False,
    )
```

profile of v0, /device:TPU:0, one launch (start us, length us, event | category | flops | bytes accessed | tf_op | source)
XLA Modules:
  0.0 1008.6 jit_solution(7018529357525210481)
XLA Ops:
  7.2 0.0 all-gather.4.cloned.1.call-start
  7.2 0.7 all-gather.4.cloned.1.call-update
  7.9 0.0 all-gather.6.cloned.1.call-start
  7.9 0.7 all-gather.6.cloned.1.call-update
  8.6 0.0 all-gather.8.cloned.1.call-start
  8.7 0.7 all-gather.8.cloned.1.call-update
  9.4 0.0 reduce-scatter.3.cloned.1.call-start
  9.4 35.9 %all-gather.4.cloned.1.call-done = bf16[512,2048]{1,0:T(8,128)(2,1)} async-done(((bf16[512,1024]{1,0:T(8,128)(2,1)}), bf16[512,2048]{1,0:T(8,128)(2,1)}) %all-gather.4.cloned.1.call-update) | async-done | bytes 2097168 | tf_op jit(solution)/shard_map/all_gather | solution.py:34
  45.4 288.4 %all-gather.6.cloned.1.call-done = bf16[4096,2048]{1,0:T(8,128)(2,1)} async-done(((bf16[4096,512]{1,0:T(8,128)(2,1)}), bf16[4096,2048]{1,0:T(8,128)(2,1)}) %all-gather.6.cloned.1.call-update) | async-done | bytes 16777232 | tf_op jit(solution)/shard_map/all_gather | solution.py:11
  333.7 15.1 %fusion = f32[512,4096]{1,0:T(8,128)} fusion(bf16[512,2048]{1,0:T(8,128)(2,1)} %all-gather.4.cloned.1.call-done, bf16[4096,2048]{1,0:T(8,128)(2,1)} %all-gather.6.cloned.1.call-done), kind=kOutput, calls=%fused_computation | convolution fusion | flops 8589934592 | bytes 27262976 | tf_op jit(solution)/shard_map/dot_general | solution.py:12
  348.8 0.0 copy-start
  348.8 0.0 reduce-scatter.3.cloned.1.call-update
  348.8 0.0 reduce-scatter.5.cloned.1.call-start
  348.9 19.1 %all-gather.8.cloned.1.call-done = bf16[512,4096]{1,0:T(8,128)(2,1)} async-done(((bf16[128,4096]{1,0:T(8,128)(2,1)}), bf16[512,4096]{1,0:T(8,128)(2,1)}) %all-gather.8.cloned.1.call-update) | async-done | bytes 4194320 | tf_op jit(solution)/shard_map/all_gather | solution.py:23
  368.0 0.0 copy-done
  368.0 21.6 %fusion.1 = f32[4096,2048]{1,0:T(8,128)} fusion(bf16[512,4096]{1,0:T(8,128)(2,1)} %all-gather.8.cloned.1.call-done, bf16[512,2048]{1,0:T(8,128)(2,1)S(1)} %copy-done), kind=kOutput, calls=%fused_computation.1 | convolution fusion | flops 8589934592 | bytes 39845888 | tf_op jit(solution)/shard_map/dot_general | solution.py:22
  389.5 0.0 reduce-scatter.5.cloned.1.call-update
  389.6 52.2 %reduce-scatter.3.cloned.1.call-done = f32[512,1024]{1,0:T(8,128)} async-done(((f32[512,4096]{1,0:T(8,128)}), f32[512,1024]{1,0:T(8,128)}) %reduce-scatter.3.cloned.1.call-update) | async-done | bytes 2097168 | tf_op jit(solution)/shard_map/reduce_scatter | solution.py:15
  441.7 1.7 convert_element_type.6
  443.5 16.9 %all_to_all.19 = bf16[4,128,1024]{2,1,0:T(8,128)(2,1)S(1)} all-to-all(bf16[4,128,1024]{2,1,0:T(8,128)(2,1)S(1)} %bitcast.8), channel_id=1, replica_groups=mesh['row'=4,'col'=4,'depth'=2] {'col'}, dimensions={0} | all-to-all | bytes 2097152 | tf_op jit(solution)/shard_map/all_to_all | solution.py:18
  460.3 1.1 copy.6
  461.4 534.8 %reduce-scatter.5.cloned.1.call-done = f32[4096,512]{1,0:T(8,128)} async-done(((f32[4096,2048]{1,0:T(8,128)}), f32[4096,512]{1,0:T(8,128)}) %reduce-scatter.5.cloned.1.call-update) | async-done | bytes 8388624 | tf_op jit(solution)/shard_map/reduce_scatter | solution.py:28
  996.1 5.9 convert_element_type.7
Async XLA Ops:
  7.2 38.2 %all-gather.4.cloned.1.call-start = ((), (), s32[]{:S(2)}) async-start(), calls=%async_computation.3 | async-start | bytes 3145728 | tf_op jit(solution)/shard_map/all_gather | solution.py:34
  7.9 325.8 %all-gather.6.cloned.1.call-start = ((), (), s32[]{:S(2)}) async-start(), calls=%async_computation.4 | async-start | bytes 20971520 | tf_op jit(solution)/shard_map/all_gather | solution.py:11
  8.6 359.3 %all-gather.8.cloned.1.call-start = ((), (), s32[]{:S(2)}) async-start(), calls=%async_computation.6 | async-start | bytes 5242880 | tf_op jit(solution)/shard_map/all_gather | solution.py:23
  9.4 432.3 %reduce-scatter.3.cloned.1.call-start = ((), (), s32[]{:S(2)}) async-start(), calls=%async_computation.5 | async-start | bytes 10485760 | tf_op jit(solution)/shard_map/reduce_scatter | solution.py:15
  348.8 19.2 %copy-start = (bf16[512,2048]{1,0:T(8,128)(2,1)S(1)}, bf16[512,2048]{1,0:T(8,128)(2,1)}, u32[]{:S(2)}) copy-start(bf16[512,2048]{1,0:T(8,128)(2,1)} %all-gather.4.cloned.1.call-done) | copy-start | bytes 6291460
  348.8 647.3 %reduce-scatter.5.cloned.1.call-start = ((), (), s32[]{:S(2)}) async-start(), calls=%async_computation.7 | async-start | bytes 41943040 | tf_op jit(solution)/shard_map/reduce_scatter | solution.py:28
Sparse Core Ops, SparseCore 0:
  9.5 35.8 all-gather.3
  46.9 286.7 all-gather.5
  335.3 32.6 all-gather.7
  370.4 71.2 reduce-scatter.2
  443.9 552.1 reduce-scatter.4
where the time goes:
time: 1010 us
  waiting for transfers between devices  932 us (92%)
  matrix products  36.6 us (4%)
  blocking collectives  16.9 us (2%)
  between operations  13.8 us (1%)
    reduce_scatter x1, waiting for transfers between devices, weight_grads(): lax.psum_scatter(partial_value, 'row', scatter_dimension=1, tiled=True)  535 us
    all_gather x1, waiting for transfers between devices, input_grads(): weight_block = lax.all_gather(weight, 'row', axis=1, tiled=True)  288 us
    reduce_scatter x1, waiting for transfers between devices, input_grads(): lax.psum_scatter(partial_value, 'col', scatter_dimension=1, tiled=True)  52.2 us
    all_gather x1, waiting for transfers between devices, per_device(): grad_block = lax.all_gather(grad_output, 'depth', axis=1, tiled=True)  35.9 us
    dot_general x1, matrix products, weight_grads(): lax.dot_general(lax.all_gather(tokens, 'col', axis=0, tiled=True), grad_b...  21.6 us
  transfers between devices with their start and end apart: 5, of which 5 were waited for; matrix products, arithmetic and copies ran while one was open for 4% of the time, Pallas kernels for 0%

commit v1 on v0

--- a/solution.py
+++ b/solution.py
@@ -8,7 +8,12 @@
 
 
 def input_grads(weight, grad_block):
-    weight_block = lax.all_gather(weight, "row", axis=1, tiled=True)
+    ring = [weight]
+    for hop in range(3):
+        ring.append(lax.ppermute(ring[-1], "row", [(dev, (dev + 1) % 4) for dev in range(4)]))
+    weight_block = jnp.roll(
+        jnp.concatenate(ring[::-1], axis=1), (lax.axis_index("row") + 1) * ring[0].shape[1], axis=1
+    )
     partial_value = lax.dot_general(
         grad_block, weight_block, last_with_last, preferred_element_type=jnp.float32
     )

time: 1010 us -> 973 us (0.963)
  waiting for transfers between devices: 932 us -> 863 us
  local copies, waits for them, and re-layouts: 1.07 us -> 30.5 us
    all_gather x1 -> x0, waiting for transfers between devices: 288 us -> none  [input_grads(): weight_block = lax.all_gather(weight, 'row', axis=1, tiled=True)]
    ppermute x0 -> x3, waiting for transfers between devices: none -> 279 us  [input_grads(): lax.ppermute(ring[-1], 'row', [(dev, (dev + 1) % 4) for dev in range(4)])]
    all_gather x1, waiting for transfers between devices: 35.9 us -> 0.01 us  [per_device(): grad_block = lax.all_gather(grad_output, 'depth', axis=1, tiled=True)]
    unnamed x2 -> x16, local copies, waits for them, and re-layouts: 0.01 us -> 28.2 us
    all_gather x1, waiting for transfers between devices: 19.1 us -> 0.02 us  [weight_grads(): lax.all_gather(tokens, 'col', axis=0, tiled=True)]
  transfers between devices with their start and end apart: 5 -> 7, of which waited for: 5 -> 5; matrix products, arithmetic and copies ran while one was open for 4% -> 7% of each run, Pallas kernels for 0% -> 0%
where the time goes in v1:
time: 973 us
  waiting for transfers between devices  863 us (89%)
  matrix products  37.3 us (4%)
  local copies, waits for them, and re-layouts  30.5 us (3%)
  blocking collectives  16.9 us (2%)
  between operations  13.8 us (1%)
    reduce_scatter x1, waiting for transfers between devices, weight_grads(): lax.psum_scatter(partial_value, 'row', scatter_dimension=1, tiled=True)  535 us
    ppermute x3, waiting for transfers between devices, input_grads(): lax.ppermute(ring[-1], 'row', [(dev, (dev + 1) % 4) for dev in range(4)])  279 us
    reduce_scatter x1, waiting for transfers between devices, input_grads(): lax.psum_scatter(partial_value, 'col', scatter_dimension=1, tiled=True)  49 us
    unnamed x16, local copies, waits for them, and re-layouts  28.2 us
    dot_general x1, matrix products, weight_grads(): lax.dot_general(lax.all_gather(tokens, 'col', axis=0, tiled=True), grad_b...  20 us
  transfers between devices with their start and end apart: 7, of which 5 were waited for; matrix products, arithmetic and copies ran while one was open for 7% of the time, Pallas kernels for 0%

profile of v1, /device:TPU:0, one launch (start us, length us, event | category | flops | bytes accessed | tf_op | source)
XLA Modules:
  0.0 972.6 jit_solution(14187249734127800834)
XLA Ops:
  7.2 3.1 collective-permute-start
  10.3 92.8 %collective-permute-done = bf16[4096,512]{1,0:T(8,128)(2,1)S(1)} collective-permute-done((bf16[4096,512]{1,0:T(8,128)(2,1)}, bf16[4096,512]{1,0:T(8,128)(2,1)S(1)}, u32[]{:S(2)}, u32[]{:S(2)}) %collective-permute-start) | collective-permute-done | bytes 4194336 | tf_op jit(solution)/shard_map/ppermute | solution.py:13
  103.1 2.0 copy-done.1
  105.1 93.6 %collective-permute-done.1 = bf16[4096,512]{1,0:T(8,128)(2,1)} collective-permute-done((bf16[4096,512]{1,0:T(8,128)(2,1)S(1)}, bf16[4096,512]{1,0:T(8,128)(2,1)}, u32[]{:S(2)}, u32[]{:S(2)}) %collective-permute-start.1) | collective-permute-done | bytes 4194336 | tf_op jit(solution)/shard_map/ppermute | solution.py:13
  198.8 0.0 all-gather.5.cloned.1.call-start
  198.9 0.7 all-gather.5.cloned.1.call-update
  199.6 92.1 %collective-permute-done.2 = bf16[4096,512]{1,0:T(8,128)(2,1)} collective-permute-done((bf16[4096,512]{1,0:T(8,128)(2,1)}, bf16[4096,512]{1,0:T(8,128)(2,1)}, u32[]{:S(2)}, u32[]{:S(2)}) %collective-permute-start.2) | collective-permute-done | bytes 4194336 | tf_op jit(solution)/shard_map/ppermute | solution.py:13
  291.8 4.5 constant_dynamic-update-slice_fusion.7
  296.2 4.5 constant_dynamic-update-slice_fusion.6
  300.7 2.3 constant_dynamic-update-slice_fusion.5
  303.0 2.3 constant_dynamic-update-slice_fusion.4
  305.4 4.5 constant_dynamic-update-slice_fusion.3
  309.8 4.5 constant_dynamic-update-slice_fusion.2
  314.3 2.3 constant_dynamic-update-slice_fusion.1
  316.7 2.3 constant_dynamic-update-slice_fusion
  318.9 17.3 %fusion.2 = f32[512,4096]{0,1:T(8,128)} fusion(bf16[512,2048]{1,0:T(8,128)(2,1)} %all-gather.3.cloned.1.call-done, bf16[4096,4096]{1,0:T(8,128)(2,1)} %constant_dynamic-update-slice_fusion, s32[]{:T(128)S(6)} %select_n.14), kind=kOutput, calls=%fused_computation.2 | convolution fusion | flops 8589934592 | bytes 27262980 | tf_op jit(solution)/shard_map/dot_general | solution.py:17
  336.3 0.2 reduce-scatter.5.cloned.1.call-start
  336.6 20.0 %fusion.6 = f32[4096,2048]{1,0:T(8,128)} fusion(bf16[512,4096]{1,0:T(8,128)(2,1)} %all-gather.5.cloned.1.call-done, bf16[512,2048]{1,0:T(8,128)(2,1)S(1)} %copy-done.3), kind=kOutput, calls=%fused_computation.14 | convolution fusion | flops 8589934592 | bytes 39845888 | tf_op jit(solution)/shard_map/dot_general | solution.py:27
  356.6 49.0 %reduce-scatter.3.cloned.1.call-done = f32[512,1024]{0,1:T(8,128)} async-done(((f32[512,4096]{0,1:T(8,128)}), f32[512,1024]{0,1:T(8,128)}) %reduce-scatter.3.cloned.1.call-update) | async-done | bytes 2097168 | tf_op jit(solution)/shard_map/reduce_scatter | solution.py:20
  405.6 1.7 copy_bitcast_fusion
  407.4 16.9 %all_to_all.19 = bf16[4,128,1024]{1,2,0:T(8,128)(2,1)S(1)} all-to-all(bf16[4,128,1024]{1,2,0:T(8,128)(2,1)S(1)} %copy_bitcast_fusion), channel_id=1, replica_groups=mesh['row'=4,'col'=4,'depth'=2] {'col'}, dimensions={0} | all-to-all | bytes 2097152 | tf_op jit(solution)/shard_map/all_to_all | solution.py:23
  424.2 1.3 copy.7
  425.5 534.6 %reduce-scatter.5.cloned.1.call-done = f32[4096,512]{1,0:T(8,128)} async-done(((f32[4096,2048]{1,0:T(8,128)}), f32[4096,512]{1,0:T(8,128)}) %reduce-scatter.5.cloned.1.call-update) | async-done | bytes 8388624 | tf_op jit(solution)/shard_map/reduce_scatter | solution.py:33
  960.1 5.9 convert_element_type.7
  (16 shorter events, 0.2 us)
Async XLA Ops:
  7.2 311.8 %all-gather.3.cloned.1.call-start = ((), (), s32[]{:S(2)}) async-start(), calls=%async_computation.3 | async-start | bytes 3145728 | tf_op jit(solution)/shard_map/all_gather | solution.py:39
  7.2 95.9 %collective-permute-start = (bf16[4096,512]{1,0:T(8,128)(2,1)}, bf16[4096,512]{1,0:T(8,128)(2,1)S(1)}, u32[]{:S(2)}, u32[]{:S(2)}) collective-permute-start(bf16[4096,512]{1,0:T(8,128)(2,1)} %param.4), channel_id=1, source_target_pairs={{0,8},{8,16},{16,24},{24,0},{1,9},{9,17},{17,25},{25,1},{2,10},{10... | collective-permute-start | bytes 12582920 | tf_op jit(solution)/shard_map/ppermute | solution.py:13
  103.1 2.0 copy-start.1
  105.1 93.6 %collective-permute-start.1 = (bf16[4096,512]{1,0:T(8,128)(2,1)S(1)}, bf16[4096,512]{1,0:T(8,128)(2,1)}, u32[]{:S(2)}, u32[]{:S(2)}) collective-permute-start(bf16[4096,512]{1,0:T(8,128)(2,1)S(1)} %collective-permute-done), channel_id=1, source_target_pairs={{0,8},{8,16},{16,24},{24,0},{1,9},{9,17},{17,25},{25,1},{2,10},{10... | collective-permute-start | bytes 12582920 | tf_op jit(solution)/shard_map/ppermute | solution.py:13
  198.8 93.0 %collective-permute-start.2 = (bf16[4096,512]{1,0:T(8,128)(2,1)}, bf16[4096,512]{1,0:T(8,128)(2,1)}, u32[]{:S(2)}, u32[]{:S(2)}) collective-permute-start(bf16[4096,512]{1,0:T(8,128)(2,1)} %collective-permute-done.1), channel_id=1, source_target_pairs={{0,8},{8,16},{16,24},{24,0},{1,9},{9,17},{17,25},{25,1},{2,10},{10... | collective-permute-start | bytes 12582920 | tf_op jit(solution)/shard_map/ppermute | solution.py:13
  198.8 137.7 %all-gather.5.cloned.1.call-start = ((), (), s32[]{:S(2)}) async-start(), calls=%async_computation.5 | async-start | bytes 5242880 | tf_op jit(solution)/shard_map/all_gather | solution.py:28
  199.6 206.1 %reduce-scatter.3.cloned.1.call-start = ((), (), s32[]{:S(2)}) async-start(), calls=%async_computation.4 | async-start | bytes 10485760 | tf_op jit(solution)/shard_map/reduce_scatter | solution.py:20
  199.6 101.1 %copy-start.2 = (bf16[4096,512]{1,0:T(8,128)(2,1)S(1)}, bf16[4096,512]{1,0:T(8,128)(2,1)}, u32[]{:S(2)}) copy-start(bf16[4096,512]{1,0:T(8,128)(2,1)} %copy-done.1) | copy-start | bytes 12582916
  199.6 103.4 %copy-start = (bf16[4096,512]{1,0:T(8,128)(2,1)S(1)}, bf16[4096,512]{1,0:T(8,128)(2,1)}, u32[]{:S(2)}) copy-start(bf16[4096,512]{1,0:T(8,128)(2,1)} %param.4) | copy-start | bytes 12582916
  318.9 17.6 %copy-start.3 = (bf16[512,2048]{1,0:T(8,128)(2,1)S(1)}, bf16[512,2048]{1,0:T(8,128)(2,1)}, u32[]{:S(2)}) copy-start(bf16[512,2048]{1,0:T(8,128)(2,1)} %all-gather.3.cloned.1.call-done) | copy-start | bytes 6291460
  336.3 623.8 %reduce-scatter.5.cloned.1.call-start = ((), (), s32[]{:S(2)}) async-start(), calls=%async_computation.6 | async-start | bytes 41943040 | tf_op jit(solution)/shard_map/reduce_scatter | solution.py:33
Sparse Core Ops, SparseCore 0:
  198.9 34.3 all-gather.2
  234.9 34.4 all-gather.4
  336.4 69.1 reduce-scatter.2
  407.8 552.2 reduce-scatter.4
